TPU v7x, 32 devices: a 4x4x1 block of a 4x4x8 slice. The times are simulated.
32 devices in a mesh: dp: 1 (over z), cy: 4 (over y), cx: 8 (over x, core).
Axes of the slice: x: 4, y: 4, z: 1, core: 2. Of those that a mesh axis runs over, the one named last changes fastest.
The devices are a block of a 4x4x8 slice.
Arguments:
- query_rows: bfloat16 [8192, 32, 128], P(('dp', 'cy', 'cx'))
- key_rows: bfloat16 [8192, 8, 128], P(('dp', 'cy', 'cx'))
- value_rows: bfloat16 [8192, 8, 128], P(('dp', 'cy', 'cx'))
- out_rows: bfloat16 [8192, 32, 128], P(('dp', 'cy', 'cx'))
- grad_out: bfloat16 [8192, 32, 128], P(('dp', 'cy', 'cx'))
- log_sum_exp: float32 [8192, 32], P(('dp', 'cy', 'cx'))
Outputs:
- output 1: bfloat16 [8192, 32, 128], P(('dp', 'cy', 'cx'))
- output 2: bfloat16 [8192, 8, 128], P(('dp', 'cy', 'cx'))
- output 3: bfloat16 [8192, 8, 128], P(('dp', 'cy', 'cx'))
All inputs are finite; a program needn't handle non-finite values.
Results may differ from a plain program's by a relative error of at most 0.00402.
Values are sent between devices in bfloat16 or wider.
A program may use at most 768 MiB of HBM per device.

v0:
```python
import math
import jax
import jax.numpy as jnp
from jax import lax
from jax.sharding import PartitionSpec as P


def block_grads(q_blk, do_blk, lse_blk, delta_blk, k_blk, v_blk, keep_mask, scaling):
    score_f32 = jnp.einsum('qkgd,skd->kqgs', q_blk, k_blk, preferred_element_type=jnp.float32) * scaling
    prob_f32 = jnp.exp(score_f32 - lse_blk[..., None])
    if keep_mask is not None:
        prob_f32 = jnp.where(keep_mask[None, :, None, :], prob_f32, 0.0)
    dprob_f32 = jnp.einsum('qkgd,skd->kqgs', do_blk, v_blk, preferred_element_type=jnp.float32)
    dscore_b16 = (prob_f32 * (dprob_f32 - delta_blk[..., None])).astype(jnp.bfloat16)
    prob_b16 = prob_f32.astype(jnp.bfloat16)
    dq_part = jnp.einsum('kqgs,skd->kqgd', dscore_b16, k_blk, preferred_element_type=jnp.float32)
    dk_part = jnp.einsum('kqgs,qkgd->ksd', dscore_b16, q_blk, preferred_element_type=jnp.float32)
    dv_part = jnp.einsum('kqgs,qkgd->ksd', prob_b16, do_blk, preferred_element_type=jnp.float32)
    return dq_part, dk_part, dv_part


def solution(mesh):
    n_cx = mesh.shape['cx']
    n_ctx = mesh.shape['cy'] * n_cx
    ctx_axes = ('cy', 'cx')
    shift_perm = [(dev_idx, (dev_idx + 1) % n_ctx) for dev_idx in range(n_ctx)]
    row_spec = P(('dp', 'cy', 'cx'), None, None)
    stat_spec = P(('dp', 'cy', 'cx'), None)

    def local_grads(query_rows, key_rows, value_rows, out_rows, grad_out, log_sum_exp):
        tok_dev, n_heads, head_dim = query_rows.shape
        kv_heads = key_rows.shape[1]
        group_size = n_heads // kv_heads
        half_tok = tok_dev // 2
        scaling = 1.0 / math.sqrt(head_dim)
        ctx_rank = lax.axis_index('cy') * n_cx + lax.axis_index('cx')
        q_grp = query_rows.reshape(tok_dev, kv_heads, group_size, head_dim)
        do_grp = grad_out.reshape(tok_dev, kv_heads, group_size, head_dim)
        lse_grp = log_sum_exp.reshape(tok_dev, kv_heads, group_size).transpose(1, 0, 2)
        delta_grp = jnp.einsum('thd,thd->th', grad_out, out_rows, preferred_element_type=jnp.float32).reshape(tok_dev, kv_heads, group_size).transpose(1, 0, 2)
        local_idx = jnp.arange(tok_dev)
        piece_id = jnp.where(local_idx < half_tok, ctx_rank, 2 * n_ctx - 1 - ctx_rank)
        own_pos = piece_id * half_tok + local_idx % half_tok
        diag_mask = own_pos[:, None] >= own_pos[None, :]
        dq_own, dk_own, dv_own = block_grads(q_grp, do_grp, lse_grp, delta_grp, key_rows, value_rows, diag_mask, scaling)

        def src_before(k_blk, v_blk):
            dq_part, dk_part, dv_part = block_grads(q_grp, do_grp, lse_grp, delta_grp, k_blk[:half_tok], v_blk[:half_tok], None, scaling)
            zero_pad = jnp.zeros_like(dk_part)
            return dq_part, jnp.concatenate([dk_part, zero_pad], axis=1), jnp.concatenate([dv_part, zero_pad], axis=1)

        def src_after(k_blk, v_blk):
            dq_part, dk_part, dv_part = block_grads(q_grp[half_tok:], do_grp[half_tok:], lse_grp[:, half_tok:], delta_grp[:, half_tok:], k_blk, v_blk, None, scaling)
            zero_pad = jnp.zeros_like(dq_part)
            return jnp.concatenate([zero_pad, dq_part], axis=1), dk_part, dv_part

        def step_body(step_idx, state):
            k_cur, v_cur, dk_cur, dv_cur, dq_cur = state
            k_cur = lax.ppermute(k_cur, ctx_axes, shift_perm)
            v_cur = lax.ppermute(v_cur, ctx_axes, shift_perm)
            dk_cur = lax.ppermute(dk_cur, ctx_axes, shift_perm)
            dv_cur = lax.ppermute(dv_cur, ctx_axes, shift_perm)
            src_rank = (ctx_rank - step_idx) % n_ctx
            dq_part, dk_part, dv_part = lax.cond(src_rank < ctx_rank, src_before, src_after, k_cur, v_cur)
            return (k_cur, v_cur, dk_cur + dk_part, dv_cur + dv_part, dq_cur + dq_part)

        k_end, v_end, dk_end, dv_end, dq_end = lax.fori_loop(1, n_ctx, step_body, (key_rows, value_rows, dk_own, dv_own, dq_own))
        dk_home = lax.ppermute(dk_end, ctx_axes, shift_perm)
        dv_home = lax.ppermute(dv_end, ctx_axes, shift_perm)
        grad_query = (dq_end * scaling).astype(jnp.bfloat16).transpose(1, 0, 2, 3).reshape(tok_dev, n_heads, head_dim)
        grad_key = (dk_home * scaling).astype(jnp.bfloat16).transpose(1, 0, 2)
        grad_value = dv_home.astype(jnp.bfloat16).transpose(1, 0, 2)
        return grad_query, grad_key, grad_value

    return jax.shard_map(local_grads, mesh=mesh, in_specs=(row_spec, row_spec, row_spec, row_spec, row_spec, stat_spec), out_specs=(row_spec, row_spec, row_spec), check_vma=False)
```

profile of v0, /device:TPU:120, one launch (start us, length us, event | category | flops | bytes accessed | tf_op | source)
XLA Modules:
  0.0 1896.9 jit_solution(2896854466799332571)
XLA Ops:
  26.6 1844.8 %while.23 = (s32[]{:T(128)}, bf16[256,8,128]{2,0,1:T(8,128)(2,1)}, bf16[256,8,128]{2,0,1:T(8,128)(2,1)}, f32[8,256,128]{2,1,0:T(8,128)}, f32[8,256,128]{2,1,0:T(...) while((s32[]{:T(128)}, bf16[256,8,128]{2,0,1:T(8,128)(2,1)}, ...), condition=%wide.region_3.4_spmd, body=%wide.region_0.3_spmd.sunk | while | flops 1352138752 | bytes 78479952 | solution.py:67
  146.8 33.0 %collective-permute-done = bf16[256,8,128]{2,0,1:T(8,128)(2,1)S(1)} collective-permute-done((bf16[256,8,128]{2,0,1:T(8,128)(2,1)}, bf16[256,8,128]{2,0,1:T(8,128)(2,1)S(1)}, u32[]{:S(2)}, u32[]{:S(2)}) %collective-permute-start) | collective-permute-done | bytes 524320 | tf_op jit(solution)/shard_map/while/body/eval_jaxpr/ppermute | solution.py:59
  206.8 33.0 %collective-permute-done = bf16[256,8,128]{2,0,1:T(8,128)(2,1)S(1)} collective-permute-done((bf16[256,8,128]{2,0,1:T(8,128)(2,1)}, bf16[256,8,128]{2,0,1:T(8,128)(2,1)S(1)}, u32[]{:S(2)}, u32[]{:S(2)}) %collective-permute-start) | collective-permute-done | bytes 524320 | tf_op jit(solution)/shard_map/while/body/eval_jaxpr/ppermute | solution.py:59
  266.7 33.0 %collective-permute-done = bf16[256,8,128]{2,0,1:T(8,128)(2,1)S(1)} collective-permute-done((bf16[256,8,128]{2,0,1:T(8,128)(2,1)}, bf16[256,8,128]{2,0,1:T(8,128)(2,1)S(1)}, u32[]{:S(2)}, u32[]{:S(2)}) %collective-permute-start) | collective-permute-done | bytes 524320 | tf_op jit(solution)/shard_map/while/body/eval_jaxpr/ppermute | solution.py:59
  326.7 33.0 %collective-permute-done = bf16[256,8,128]{2,0,1:T(8,128)(2,1)S(1)} collective-permute-done((bf16[256,8,128]{2,0,1:T(8,128)(2,1)}, bf16[256,8,128]{2,0,1:T(8,128)(2,1)S(1)}, u32[]{:S(2)}, u32[]{:S(2)}) %collective-permute-start) | collective-permute-done | bytes 524320 | tf_op jit(solution)/shard_map/while/body/eval_jaxpr/ppermute | solution.py:59
  386.7 33.0 %collective-permute-done = bf16[256,8,128]{2,0,1:T(8,128)(2,1)S(1)} collective-permute-done((bf16[256,8,128]{2,0,1:T(8,128)(2,1)}, bf16[256,8,128]{2,0,1:T(8,128)(2,1)S(1)}, u32[]{:S(2)}, u32[]{:S(2)}) %collective-permute-start) | collective-permute-done | bytes 524320 | tf_op jit(solution)/shard_map/while/body/eval_jaxpr/ppermute | solution.py:59
  446.7 33.0 %collective-permute-done = bf16[256,8,128]{2,0,1:T(8,128)(2,1)S(1)} collective-permute-done((bf16[256,8,128]{2,0,1:T(8,128)(2,1)}, bf16[256,8,128]{2,0,1:T(8,128)(2,1)S(1)}, u32[]{:S(2)}, u32[]{:S(2)}) %collective-permute-start) | collective-permute-done | bytes 524320 | tf_op jit(solution)/shard_map/while/body/eval_jaxpr/ppermute | solution.py:59
  506.7 33.0 %collective-permute-done = bf16[256,8,128]{2,0,1:T(8,128)(2,1)S(1)} collective-permute-done((bf16[256,8,128]{2,0,1:T(8,128)(2,1)}, bf16[256,8,128]{2,0,1:T(8,128)(2,1)S(1)}, u32[]{:S(2)}, u32[]{:S(2)}) %collective-permute-start) | collective-permute-done | bytes 524320 | tf_op jit(solution)/shard_map/while/body/eval_jaxpr/ppermute | solution.py:59
  566.7 33.0 %collective-permute-done = bf16[256,8,128]{2,0,1:T(8,128)(2,1)S(1)} collective-permute-done((bf16[256,8,128]{2,0,1:T(8,128)(2,1)}, bf16[256,8,128]{2,0,1:T(8,128)(2,1)S(1)}, u32[]{:S(2)}, u32[]{:S(2)}) %collective-permute-start) | collective-permute-done | bytes 524320 | tf_op jit(solution)/shard_map/while/body/eval_jaxpr/ppermute | solution.py:59
  626.7 33.0 %collective-permute-done = bf16[256,8,128]{2,0,1:T(8,128)(2,1)S(1)} collective-permute-done((bf16[256,8,128]{2,0,1:T(8,128)(2,1)}, bf16[256,8,128]{2,0,1:T(8,128)(2,1)S(1)}, u32[]{:S(2)}, u32[]{:S(2)}) %collective-permute-start) | collective-permute-done | bytes 524320 | tf_op jit(solution)/shard_map/while/body/eval_jaxpr/ppermute | solution.py:59
  686.7 33.0 %collective-permute-done = bf16[256,8,128]{2,0,1:T(8,128)(2,1)S(1)} collective-permute-done((bf16[256,8,128]{2,0,1:T(8,128)(2,1)}, bf16[256,8,128]{2,0,1:T(8,128)(2,1)S(1)}, u32[]{:S(2)}, u32[]{:S(2)}) %collective-permute-start) | collective-permute-done | bytes 524320 | tf_op jit(solution)/shard_map/while/body/eval_jaxpr/ppermute | solution.py:59
  746.7 33.0 %collective-permute-done = bf16[256,8,128]{2,0,1:T(8,128)(2,1)S(1)} collective-permute-done((bf16[256,8,128]{2,0,1:T(8,128)(2,1)}, bf16[256,8,128]{2,0,1:T(8,128)(2,1)S(1)}, u32[]{:S(2)}, u32[]{:S(2)}) %collective-permute-start) | collective-permute-done | bytes 524320 | tf_op jit(solution)/shard_map/while/body/eval_jaxpr/ppermute | solution.py:59
  806.7 33.0 %collective-permute-done = bf16[256,8,128]{2,0,1:T(8,128)(2,1)S(1)} collective-permute-done((bf16[256,8,128]{2,0,1:T(8,128)(2,1)}, bf16[256,8,128]{2,0,1:T(8,128)(2,1)S(1)}, u32[]{:S(2)}, u32[]{:S(2)}) %collective-permute-start) | collective-permute-done | bytes 524320 | tf_op jit(solution)/shard_map/while/body/eval_jaxpr/ppermute | solution.py:59
  866.7 33.0 %collective-permute-done = bf16[256,8,128]{2,0,1:T(8,128)(2,1)S(1)} collective-permute-done((bf16[256,8,128]{2,0,1:T(8,128)(2,1)}, bf16[256,8,128]{2,0,1:T(8,128)(2,1)S(1)}, u32[]{:S(2)}, u32[]{:S(2)}) %collective-permute-start) | collective-permute-done | bytes 524320 | tf_op jit(solution)/shard_map/while/body/eval_jaxpr/ppermute | solution.py:59
  926.6 33.0 %collective-permute-done = bf16[256,8,128]{2,0,1:T(8,128)(2,1)S(1)} collective-permute-done((bf16[256,8,128]{2,0,1:T(8,128)(2,1)}, bf16[256,8,128]{2,0,1:T(8,128)(2,1)S(1)}, u32[]{:S(2)}, u32[]{:S(2)}) %collective-permute-start) | collective-permute-done | bytes 524320 | tf_op jit(solution)/shard_map/while/body/eval_jaxpr/ppermute | solution.py:59
  986.6 33.0 %collective-permute-done = bf16[256,8,128]{2,0,1:T(8,128)(2,1)S(1)} collective-permute-done((bf16[256,8,128]{2,0,1:T(8,128)(2,1)}, bf16[256,8,128]{2,0,1:T(8,128)(2,1)S(1)}, u32[]{:S(2)}, u32[]{:S(2)}) %collective-permute-start) | collective-permute-done | bytes 524320 | tf_op jit(solution)/shard_map/while/body/eval_jaxpr/ppermute | solution.py:59
  1046.6 33.0 %collective-permute-done = bf16[256,8,128]{2,0,1:T(8,128)(2,1)S(1)} collective-permute-done((bf16[256,8,128]{2,0,1:T(8,128)(2,1)}, bf16[256,8,128]{2,0,1:T(8,128)(2,1)S(1)}, u32[]{:S(2)}, u32[]{:S(2)}) %collective-permute-start) | collective-permute-done | bytes 524320 | tf_op jit(solution)/shard_map/while/body/eval_jaxpr/ppermute | solution.py:59
  1106.6 33.0 %collective-permute-done = bf16[256,8,128]{2,0,1:T(8,128)(2,1)S(1)} collective-permute-done((bf16[256,8,128]{2,0,1:T(8,128)(2,1)}, bf16[256,8,128]{2,0,1:T(8,128)(2,1)S(1)}, u32[]{:S(2)}, u32[]{:S(2)}) %collective-permute-start) | collective-permute-done | bytes 524320 | tf_op jit(solution)/shard_map/while/body/eval_jaxpr/ppermute | solution.py:59
  1166.6 33.0 %collective-permute-done = bf16[256,8,128]{2,0,1:T(8,128)(2,1)S(1)} collective-permute-done((bf16[256,8,128]{2,0,1:T(8,128)(2,1)}, bf16[256,8,128]{2,0,1:T(8,128)(2,1)S(1)}, u32[]{:S(2)}, u32[]{:S(2)}) %collective-permute-start) | collective-permute-done | bytes 524320 | tf_op jit(solution)/shard_map/while/body/eval_jaxpr/ppermute | solution.py:59
  1226.6 33.0 %collective-permute-done = bf16[256,8,128]{2,0,1:T(8,128)(2,1)S(1)} collective-permute-done((bf16[256,8,128]{2,0,1:T(8,128)(2,1)}, bf16[256,8,128]{2,0,1:T(8,128)(2,1)S(1)}, u32[]{:S(2)}, u32[]{:S(2)}) %collective-permute-start) | collective-permute-done | bytes 524320 | tf_op jit(solution)/shard_map/while/body/eval_jaxpr/ppermute | solution.py:59
  1466.6 33.0 %collective-permute-done = bf16[256,8,128]{2,0,1:T(8,128)(2,1)S(1)} collective-permute-done((bf16[256,8,128]{2,0,1:T(8,128)(2,1)}, bf16[256,8,128]{2,0,1:T(8,128)(2,1)S(1)}, u32[]{:S(2)}, u32[]{:S(2)}) %collective-permute-start) | collective-permute-done | bytes 524320 | tf_op jit(solution)/shard_map/while/body/eval_jaxpr/ppermute | solution.py:59
  1582.3 33.0 %collective-permute-done = bf16[256,8,128]{2,0,1:T(8,128)(2,1)S(1)} collective-permute-done((bf16[256,8,128]{2,0,1:T(8,128)(2,1)}, bf16[256,8,128]{2,0,1:T(8,128)(2,1)S(1)}, u32[]{:S(2)}, u32[]{:S(2)}) %collective-permute-start) | collective-permute-done | bytes 524320 | tf_op jit(solution)/shard_map/while/body/eval_jaxpr/ppermute | solution.py:59
  1698.0 33.0 %collective-permute-done = bf16[256,8,128]{2,0,1:T(8,128)(2,1)S(1)} collective-permute-done((bf16[256,8,128]{2,0,1:T(8,128)(2,1)}, bf16[256,8,128]{2,0,1:T(8,128)(2,1)S(1)}, u32[]{:S(2)}, u32[]{:S(2)}) %collective-permute-start) | collective-permute-done | bytes 524320 | tf_op jit(solution)/shard_map/while/body/eval_jaxpr/ppermute | solution.py:59
  1813.7 33.0 %collective-permute-done = bf16[256,8,128]{2,0,1:T(8,128)(2,1)S(1)} collective-permute-done((bf16[256,8,128]{2,0,1:T(8,128)(2,1)}, bf16[256,8,128]{2,0,1:T(8,128)(2,1)S(1)}, u32[]{:S(2)}, u32[]{:S(2)}) %collective-permute-start) | collective-permute-done | bytes 524320 | tf_op jit(solution)/shard_map/while/body/eval_jaxpr/ppermute | solution.py:59
  (732 shorter events, 1429.8 us)
Async XLA Ops:
  26.6 57.6 %collective-permute-start.2 = (f32[8,256,128]{2,1,0:T(8,128)}, f32[8,256,128]{2,1,0:T(8,128)}, u32[]{:S(2)}, u32[]{:S(2)}) collective-permute-start(f32[8,256,128]{2,1,0:T(8,128)} %get-tuple-element.442), channel_id=1, source_target_pairs={{0,1},{1,2},{2,3},{3,4},{4,5},{5,6},{6,7},{7,8},{8,9},{9,10},{10,1... | collective-permute-start | bytes 3145736 | tf_op jit(solution)/shard_map/while/body/eval_jaxpr/ppermute | solution.py:61
  86.6 57.6 %collective-permute-start.2 = (f32[8,256,128]{2,1,0:T(8,128)}, f32[8,256,128]{2,1,0:T(8,128)}, u32[]{:S(2)}, u32[]{:S(2)}) collective-permute-start(f32[8,256,128]{2,1,0:T(8,128)} %get-tuple-element.442), channel_id=1, source_target_pairs={{0,1},{1,2},{2,3},{3,4},{4,5},{5,6},{6,7},{7,8},{8,9},{9,10},{10,1... | collective-permute-start | bytes 3145736 | tf_op jit(solution)/shard_map/while/body/eval_jaxpr/ppermute | solution.py:61
  146.6 57.6 %collective-permute-start.2 = (f32[8,256,128]{2,1,0:T(8,128)}, f32[8,256,128]{2,1,0:T(8,128)}, u32[]{:S(2)}, u32[]{:S(2)}) collective-permute-start(f32[8,256,128]{2,1,0:T(8,128)} %get-tuple-element.442), channel_id=1, source_target_pairs={{0,1},{1,2},{2,3},{3,4},{4,5},{5,6},{6,7},{7,8},{8,9},{9,10},{10,1... | collective-permute-start | bytes 3145736 | tf_op jit(solution)/shard_map/while/body/eval_jaxpr/ppermute | solution.py:61
  206.6 57.6 %collective-permute-start.2 = (f32[8,256,128]{2,1,0:T(8,128)}, f32[8,256,128]{2,1,0:T(8,128)}, u32[]{:S(2)}, u32[]{:S(2)}) collective-permute-start(f32[8,256,128]{2,1,0:T(8,128)} %get-tuple-element.442), channel_id=1, source_target_pairs={{0,1},{1,2},{2,3},{3,4},{4,5},{5,6},{6,7},{7,8},{8,9},{9,10},{10,1... | collective-permute-start | bytes 3145736 | tf_op jit(solution)/shard_map/while/body/eval_jaxpr/ppermute | solution.py:61
  266.6 57.6 %collective-permute-start.2 = (f32[8,256,128]{2,1,0:T(8,128)}, f32[8,256,128]{2,1,0:T(8,128)}, u32[]{:S(2)}, u32[]{:S(2)}) collective-permute-start(f32[8,256,128]{2,1,0:T(8,128)} %get-tuple-element.442), channel_id=1, source_target_pairs={{0,1},{1,2},{2,3},{3,4},{4,5},{5,6},{6,7},{7,8},{8,9},{9,10},{10,1... | collective-permute-start | bytes 3145736 | tf_op jit(solution)/shard_map/while/body/eval_jaxpr/ppermute | solution.py:61
  326.6 57.6 %collective-permute-start.2 = (f32[8,256,128]{2,1,0:T(8,128)}, f32[8,256,128]{2,1,0:T(8,128)}, u32[]{:S(2)}, u32[]{:S(2)}) collective-permute-start(f32[8,256,128]{2,1,0:T(8,128)} %get-tuple-element.442), channel_id=1, source_target_pairs={{0,1},{1,2},{2,3},{3,4},{4,5},{5,6},{6,7},{7,8},{8,9},{9,10},{10,1... | collective-permute-start | bytes 3145736 | tf_op jit(solution)/shard_map/while/body/eval_jaxpr/ppermute | solution.py:61
  386.6 57.6 %collective-permute-start.2 = (f32[8,256,128]{2,1,0:T(8,128)}, f32[8,256,128]{2,1,0:T(8,128)}, u32[]{:S(2)}, u32[]{:S(2)}) collective-permute-start(f32[8,256,128]{2,1,0:T(8,128)} %get-tuple-element.442), channel_id=1, source_target_pairs={{0,1},{1,2},{2,3},{3,4},{4,5},{5,6},{6,7},{7,8},{8,9},{9,10},{10,1... | collective-permute-start | bytes 3145736 | tf_op jit(solution)/shard_map/while/body/eval_jaxpr/ppermute | solution.py:61
  446.6 57.6 %collective-permute-start.2 = (f32[8,256,128]{2,1,0:T(8,128)}, f32[8,256,128]{2,1,0:T(8,128)}, u32[]{:S(2)}, u32[]{:S(2)}) collective-permute-start(f32[8,256,128]{2,1,0:T(8,128)} %get-tuple-element.442), channel_id=1, source_target_pairs={{0,1},{1,2},{2,3},{3,4},{4,5},{5,6},{6,7},{7,8},{8,9},{9,10},{10,1... | collective-permute-start | bytes 3145736 | tf_op jit(solution)/shard_map/while/body/eval_jaxpr/ppermute | solution.py:61
  506.5 57.6 %collective-permute-start.2 = (f32[8,256,128]{2,1,0:T(8,128)}, f32[8,256,128]{2,1,0:T(8,128)}, u32[]{:S(2)}, u32[]{:S(2)}) collective-permute-start(f32[8,256,128]{2,1,0:T(8,128)} %get-tuple-element.442), channel_id=1, source_target_pairs={{0,1},{1,2},{2,3},{3,4},{4,5},{5,6},{6,7},{7,8},{8,9},{9,10},{10,1... | collective-permute-start | bytes 3145736 | tf_op jit(solution)/shard_map/while/body/eval_jaxpr/ppermute | solution.py:61
  566.5 57.6 %collective-permute-start.2 = (f32[8,256,128]{2,1,0:T(8,128)}, f32[8,256,128]{2,1,0:T(8,128)}, u32[]{:S(2)}, u32[]{:S(2)}) collective-permute-start(f32[8,256,128]{2,1,0:T(8,128)} %get-tuple-element.442), channel_id=1, source_target_pairs={{0,1},{1,2},{2,3},{3,4},{4,5},{5,6},{6,7},{7,8},{8,9},{9,10},{10,1... | collective-permute-start | bytes 3145736 | tf_op jit(solution)/shard_map/while/body/eval_jaxpr/ppermute | solution.py:61
  626.5 57.6 %collective-permute-start.2 = (f32[8,256,128]{2,1,0:T(8,128)}, f32[8,256,128]{2,1,0:T(8,128)}, u32[]{:S(2)}, u32[]{:S(2)}) collective-permute-start(f32[8,256,128]{2,1,0:T(8,128)} %get-tuple-element.442), channel_id=1, source_target_pairs={{0,1},{1,2},{2,3},{3,4},{4,5},{5,6},{6,7},{7,8},{8,9},{9,10},{10,1... | collective-permute-start | bytes 3145736 | tf_op jit(solution)/shard_map/while/body/eval_jaxpr/ppermute | solution.py:61
  686.5 57.6 %collective-permute-start.2 = (f32[8,256,128]{2,1,0:T(8,128)}, f32[8,256,128]{2,1,0:T(8,128)}, u32[]{:S(2)}, u32[]{:S(2)}) collective-permute-start(f32[8,256,128]{2,1,0:T(8,128)} %get-tuple-element.442), channel_id=1, source_target_pairs={{0,1},{1,2},{2,3},{3,4},{4,5},{5,6},{6,7},{7,8},{8,9},{9,10},{10,1... | collective-permute-start | bytes 3145736 | tf_op jit(solution)/shard_map/while/body/eval_jaxpr/ppermute | solution.py:61
  746.5 57.6 %collective-permute-start.2 = (f32[8,256,128]{2,1,0:T(8,128)}, f32[8,256,128]{2,1,0:T(8,128)}, u32[]{:S(2)}, u32[]{:S(2)}) collective-permute-start(f32[8,256,128]{2,1,0:T(8,128)} %get-tuple-element.442), channel_id=1, source_target_pairs={{0,1},{1,2},{2,3},{3,4},{4,5},{5,6},{6,7},{7,8},{8,9},{9,10},{10,1... | collective-permute-start | bytes 3145736 | tf_op jit(solution)/shard_map/while/body/eval_jaxpr/ppermute | solution.py:61
  806.5 57.6 %collective-permute-start.2 = (f32[8,256,128]{2,1,0:T(8,128)}, f32[8,256,128]{2,1,0:T(8,128)}, u32[]{:S(2)}, u32[]{:S(2)}) collective-permute-start(f32[8,256,128]{2,1,0:T(8,128)} %get-tuple-element.442), channel_id=1, source_target_pairs={{0,1},{1,2},{2,3},{3,4},{4,5},{5,6},{6,7},{7,8},{8,9},{9,10},{10,1... | collective-permute-start | bytes 3145736 | tf_op jit(solution)/shard_map/while/body/eval_jaxpr/ppermute | solution.py:61
  866.5 57.6 %collective-permute-start.2 = (f32[8,256,128]{2,1,0:T(8,128)}, f32[8,256,128]{2,1,0:T(8,128)}, u32[]{:S(2)}, u32[]{:S(2)}) collective-permute-start(f32[8,256,128]{2,1,0:T(8,128)} %get-tuple-element.442), channel_id=1, source_target_pairs={{0,1},{1,2},{2,3},{3,4},{4,5},{5,6},{6,7},{7,8},{8,9},{9,10},{10,1... | collective-permute-start | bytes 3145736 | tf_op jit(solution)/shard_map/while/body/eval_jaxpr/ppermute | solution.py:61
  926.5 57.6 %collective-permute-start.2 = (f32[8,256,128]{2,1,0:T(8,128)}, f32[8,256,128]{2,1,0:T(8,128)}, u32[]{:S(2)}, u32[]{:S(2)}) collective-permute-start(f32[8,256,128]{2,1,0:T(8,128)} %get-tuple-element.442), channel_id=1, source_target_pairs={{0,1},{1,2},{2,3},{3,4},{4,5},{5,6},{6,7},{7,8},{8,9},{9,10},{10,1... | collective-permute-start | bytes 3145736 | tf_op jit(solution)/shard_map/while/body/eval_jaxpr/ppermute | solution.py:61
  986.5 57.6 %collective-permute-start.2 = (f32[8,256,128]{2,1,0:T(8,128)}, f32[8,256,128]{2,1,0:T(8,128)}, u32[]{:S(2)}, u32[]{:S(2)}) collective-permute-start(f32[8,256,128]{2,1,0:T(8,128)} %get-tuple-element.442), channel_id=1, source_target_pairs={{0,1},{1,2},{2,3},{3,4},{4,5},{5,6},{6,7},{7,8},{8,9},{9,10},{10,1... | collective-permute-start | bytes 3145736 | tf_op jit(solution)/shard_map/while/body/eval_jaxpr/ppermute | solution.py:61
  1046.5 57.6 %collective-permute-start.2 = (f32[8,256,128]{2,1,0:T(8,128)}, f32[8,256,128]{2,1,0:T(8,128)}, u32[]{:S(2)}, u32[]{:S(2)}) collective-permute-start(f32[8,256,128]{2,1,0:T(8,128)} %get-tuple-element.442), channel_id=1, source_target_pairs={{0,1},{1,2},{2,3},{3,4},{4,5},{5,6},{6,7},{7,8},{8,9},{9,10},{10,1... | collective-permute-start | bytes 3145736 | tf_op jit(solution)/shard_map/while/body/eval_jaxpr/ppermute | solution.py:61
  1106.5 57.6 %collective-permute-start.2 = (f32[8,256,128]{2,1,0:T(8,128)}, f32[8,256,128]{2,1,0:T(8,128)}, u32[]{:S(2)}, u32[]{:S(2)}) collective-permute-start(f32[8,256,128]{2,1,0:T(8,128)} %get-tuple-element.442), channel_id=1, source_target_pairs={{0,1},{1,2},{2,3},{3,4},{4,5},{5,6},{6,7},{7,8},{8,9},{9,10},{10,1... | collective-permute-start | bytes 3145736 | tf_op jit(solution)/shard_map/while/body/eval_jaxpr/ppermute | solution.py:61
  1166.5 57.6 %collective-permute-start.2 = (f32[8,256,128]{2,1,0:T(8,128)}, f32[8,256,128]{2,1,0:T(8,128)}, u32[]{:S(2)}, u32[]{:S(2)}) collective-permute-start(f32[8,256,128]{2,1,0:T(8,128)} %get-tuple-element.442), channel_id=1, source_target_pairs={{0,1},{1,2},{2,3},{3,4},{4,5},{5,6},{6,7},{7,8},{8,9},{9,10},{10,1... | collective-permute-start | bytes 3145736 | tf_op jit(solution)/shard_map/while/body/eval_jaxpr/ppermute | solution.py:61
  1226.4 57.6 %collective-permute-start.2 = (f32[8,256,128]{2,1,0:T(8,128)}, f32[8,256,128]{2,1,0:T(8,128)}, u32[]{:S(2)}, u32[]{:S(2)}) collective-permute-start(f32[8,256,128]{2,1,0:T(8,128)} %get-tuple-element.442), channel_id=1, source_target_pairs={{0,1},{1,2},{2,3},{3,4},{4,5},{5,6},{6,7},{7,8},{8,9},{9,10},{10,1... | collective-permute-start | bytes 3145736 | tf_op jit(solution)/shard_map/while/body/eval_jaxpr/ppermute | solution.py:61
  1286.4 57.6 %collective-permute-start.2 = (f32[8,256,128]{2,1,0:T(8,128)}, f32[8,256,128]{2,1,0:T(8,128)}, u32[]{:S(2)}, u32[]{:S(2)}) collective-permute-start(f32[8,256,128]{2,1,0:T(8,128)} %get-tuple-element.442), channel_id=1, source_target_pairs={{0,1},{1,2},{2,3},{3,4},{4,5},{5,6},{6,7},{7,8},{8,9},{9,10},{10,1... | collective-permute-start | bytes 3145736 | tf_op jit(solution)/shard_map/while/body/eval_jaxpr/ppermute | solution.py:61
  1346.4 57.6 %collective-permute-start.2 = (f32[8,256,128]{2,1,0:T(8,128)}, f32[8,256,128]{2,1,0:T(8,128)}, u32[]{:S(2)}, u32[]{:S(2)}) collective-permute-start(f32[8,256,128]{2,1,0:T(8,128)} %get-tuple-element.442), channel_id=1, source_target_pairs={{0,1},{1,2},{2,3},{3,4},{4,5},{5,6},{6,7},{7,8},{8,9},{9,10},{10,1... | collective-permute-start | bytes 3145736 | tf_op jit(solution)/shard_map/while/body/eval_jaxpr/ppermute | solution.py:61
  1406.4 57.6 %collective-permute-start.2 = (f32[8,256,128]{2,1,0:T(8,128)}, f32[8,256,128]{2,1,0:T(8,128)}, u32[]{:S(2)}, u32[]{:S(2)}) collective-permute-start(f32[8,256,128]{2,1,0:T(8,128)} %get-tuple-element.442), channel_id=1, source_target_pairs={{0,1},{1,2},{2,3},{3,4},{4,5},{5,6},{6,7},{7,8},{8,9},{9,10},{10,1... | collective-permute-start | bytes 3145736 | tf_op jit(solution)/shard_map/while/body/eval_jaxpr/ppermute | solution.py:61
  (138 other events, 4420.0 us)
where the time goes:
time: 1900 us
  waiting for transfers between devices  1210 us (64%)
  other arithmetic  303 us (16%)
  matrix products  276 us (15%)
  local copies, waits for them, and re-layouts  97.6 us (5%)
    ppermute x31, waiting for transfers between devices, step_body(): k_cur = lax.ppermute(k_cur, ctx_axes, shift_perm)  1020 us
    add x93, other arithmetic, step_body(): return (k_cur, v_cur, dk_cur + dk_part, dv_cur + dv_part, dq_cur + dq_part)  296 us
    ppermute x31, waiting for transfers between devices, step_body(): v_cur = lax.ppermute(v_cur, ctx_axes, shift_perm)  174 us
    dot_general x32, matrix products, block_grads(): jnp.einsum('kqgs,qkgd->ksd', prob_b16, do_blk, preferred_element_type=jnp...  125 us
    dot_general x32, matrix products, block_grads(): jnp.einsum('qkgd,skd->kqgs', do_blk, v_blk, preferred_element_type=jnp.fl...  76 us
    while x62, local copies, waits for them, and re-layouts  49.1 us
  transfers between devices with their start and end apart: 126, of which 63 were waited for; matrix products, arithmetic and copies ran while one was open for 29% of the time, Pallas kernels for 0%

commit v1 on v0

v1 whole, which is shorter than its diff:
```python
import functools
import math
import jax
import jax.numpy as jnp
from jax import lax
from jax.experimental import pallas as pl
from jax.experimental.pallas import tpu as pltpu
from jax.sharding import PartitionSpec as P

TK = 256
TQ = 512
LOG2E = 1.4426950408889634


def grad_kernel(n_row, n_src, group, scaling, rows_ref, stats_ref, kv_ref, dq_ref, dkv_ref, dqt_ref):
    my_row = lax.axis_index('cy')
    tok, dim = rows_ref.shape[3], rows_ref.shape[4]
    chunk = n_src * tok
    k_src = TK // tok
    dkv_ref[...] = jnp.zeros_like(dkv_ref)
    dqt_ref[...] = jnp.zeros_like(dqt_ref)
    s_mul = jnp.float32(scaling * LOG2E)

    def tile(head, q_half, q_first, q_n, row, k_half, k_first, k_n, mask):
        ks = pl.ds(k_first, k_n)
        qs = pl.ds(q_first, q_n)
        k_t = kv_ref[row, ks, 0, k_half].reshape(k_n * tok, dim)
        v_t = kv_ref[row, ks, 1, k_half].reshape(k_n * tok, dim)
        q_t = rows_ref[qs, head, q_half].reshape(q_n * tok, dim)
        do_t = rows_ref[qs, group + head, q_half].reshape(q_n * tok, dim)
        lse = jnp.concatenate([stats_ref[q_first + i, q_half, pl.ds(head, 1), :] for i in range(q_n)], axis=1)
        delta = jnp.concatenate([stats_ref[q_first + i, q_half, pl.ds(group + head, 1), :] for i in range(q_n)], axis=1)
        nt = (((1,), (1,)), ((), ()))
        s_t = lax.dot_general(k_t, q_t, nt, preferred_element_type=jnp.float32)
        p_t = jnp.exp2(s_t * s_mul - lse)
        if mask is not None:
            p_t = jnp.where(mask, p_t, 0.0)
        dp_t = lax.dot_general(v_t, do_t, nt, preferred_element_type=jnp.float32)
        ds_t = (p_t * (dp_t - delta)).astype(jnp.bfloat16)
        p_b = p_t.astype(jnp.bfloat16)
        dv = jnp.dot(p_b, do_t, preferred_element_type=jnp.float32)
        dk = jnp.dot(ds_t, q_t, preferred_element_type=jnp.float32)
        dqt = lax.dot_general(k_t, ds_t, (((0,), (0,)), ((), ())), preferred_element_type=jnp.float32)
        dkv_ref[row, ks, 0, k_half] += dk.reshape(k_n, tok, dim)
        dkv_ref[row, ks, 1, k_half] += dv.reshape(k_n, tok, dim)
        lanes = pl.ds(pl.multiple_of(q_first * tok, q_n * tok), q_n * tok)
        dqt_ref[head, q_half, :, lanes] += dqt

    q_n = TQ // tok
    n_qt = n_src // q_n
    n_kt = n_src // k_src
    n_pairs = 2 * n_row - 1

    def full_step(idx, carry):
        kt = lax.rem(idx, n_kt)
        head = lax.rem(lax.div(idx, n_kt), group)
        pair = lax.div(idx, n_kt * group)
        other = lax.rem(my_row + 1 + lax.max(pair - n_row, 0), n_row)
        before = other < my_row
        first = pair < n_row
        row = jnp.where(first, pair, other)
        q_half = jnp.where(jnp.logical_or(first, jnp.logical_not(before)), 1, 0)
        k_half = jnp.where(jnp.logical_or(first, before), 0, 1)
        for qt in range(n_qt):
            tile(head, q_half, qt * q_n, q_n, row, k_half, kt * k_src, k_src, None)
        return carry

    lax.fori_loop(0, n_pairs * group * n_kt, full_step, 0)

    def diag_step(idx, carry):
        kt = lax.rem(idx, n_kt)
        head = lax.rem(lax.div(idx, n_kt), group)
        half = lax.div(idx, n_kt * group)
        low = jnp.where(half == 0, kt, 0)
        high = jnp.where(half == 0, n_kt, kt + 1)

        def inner(qt, c):
            q_i = lax.broadcasted_iota(jnp.int32, (TK, TK), 1)
            k_i = lax.broadcasted_iota(jnp.int32, (TK, TK), 0)
            q_pc = qt * k_src + q_i // tok
            k_pc = kt * k_src + k_i // tok
            q_pc = jnp.where(half == 0, q_pc, n_src - 1 - q_pc)
            k_pc = jnp.where(half == 0, k_pc, n_src - 1 - k_pc)
            mask = q_pc * tok + lax.rem(q_i, tok) >= k_pc * tok + lax.rem(k_i, tok)
            tile(head, half, qt * k_src, k_src, my_row, half, kt * k_src, k_src, mask)
            return c

        return lax.fori_loop(low, high, inner, carry)

    lax.fori_loop(0, 2 * group * n_kt, diag_step, 0)

    def out_step(idx, carry):
        src = lax.rem(idx, n_src)
        head = lax.rem(lax.div(idx, n_src), group)
        half = lax.div(idx, n_src * group)
        blk = dqt_ref[head, half, :, pl.ds(pl.multiple_of(src * tok, tok), tok)]
        dq_ref[src, head, half] = (jnp.transpose(blk, (1, 0)) * scaling).astype(jnp.bfloat16)
        return carry

    lax.fori_loop(0, 2 * group * n_src, out_step, 0)


def solution(mesh):
    n_row = mesh.shape['cy']
    n_cx = mesh.shape['cx']
    row_spec = P(('dp', 'cy', 'cx'), None, None)
    stat_spec = P(('dp', 'cy', 'cx'), None)

    def local_grads(query_rows, key_rows, value_rows, out_rows, grad_out, log_sum_exp):
        tok_dev, n_heads, dim = query_rows.shape
        kv_heads = key_rows.shape[1]
        group = n_heads // kv_heads
        tok = tok_dev // 2
        scaling = 1.0 / math.sqrt(dim)
        assert kv_heads == n_cx
        delta = jnp.einsum('thd,thd->th', grad_out, out_rows, preferred_element_type=jnp.float32)

        def by_head(x, per):
            return x.reshape(2, tok, kv_heads, per, dim).transpose(2, 3, 0, 1, 4)

        send = jnp.concatenate([by_head(query_rows, group), by_head(grad_out, group), by_head(key_rows, 1), by_head(value_rows, 1)], axis=1)
        stats = jnp.concatenate([(log_sum_exp * LOG2E).reshape(2, tok, kv_heads, group), delta.reshape(2, tok, kv_heads, group)], axis=3).transpose(2, 0, 3, 1)
        rows = lax.all_to_all(send, 'cx', 0, 0, tiled=True)
        stats = lax.all_to_all(stats, 'cx', 0, 0, tiled=True)
        kv = lax.all_gather(rows[:, 2 * group:], 'cy', axis=0)
        vm = pl.BlockSpec(memory_space=pltpu.VMEM)
        dq, dkv = pl.pallas_call(
            functools.partial(grad_kernel, n_row, n_cx, group, scaling),
            out_shape=(jax.ShapeDtypeStruct((n_cx, group, 2, tok, dim), jnp.bfloat16), jax.ShapeDtypeStruct((n_row, n_cx, 2, 2, tok, dim), jnp.float32)),
            in_specs=[vm] * 3,
            out_specs=(vm, vm),
            scratch_shapes=[pltpu.VMEM((group, 2, dim, n_cx * tok), jnp.float32)],
            compiler_params=pltpu.CompilerParams(vmem_limit_bytes=60 * 1024 * 1024),
            name='grad_kernel',
        )(rows, stats, kv)
        dkv = lax.psum_scatter(dkv, 'cy', scatter_dimension=0)
        dk = (dkv[:, 0] * scaling).astype(jnp.bfloat16)
        dv = dkv[:, 1].astype(jnp.bfloat16)
        back = jnp.concatenate([dq, dk[:, None], dv[:, None]], axis=1)
        back = lax.all_to_all(back, 'cx', 0, 0, tiled=True)

        def by_tok(x):
            return x.transpose(2, 3, 0, 1, 4).reshape(tok_dev, -1, dim)

        return by_tok(back[:, :group]), by_tok(back[:, group:group + 1]), by_tok(back[:, group + 1:])

    return jax.shard_map(local_grads, mesh=mesh, in_specs=(row_spec,) * 5 + (stat_spec,), out_specs=(row_spec,) * 3, check_vma=False)
```

time: 1900 us -> 405 us (0.21)
  waiting for transfers between devices: 1210 us -> 110 us
  other arithmetic: 303 us -> 5.36 us
  matrix products: 276 us -> 0 us
  Pallas kernels: 0 us -> 139 us
  blocking collectives: 0 us -> 117 us
  local copies, waits for them, and re-layouts: 97.6 us -> 15.7 us
    ppermute x126 -> x0, waiting for transfers between devices: 1210 us -> none  [the longest x31 1020 us: step_body(): k_cur = lax.ppermute(k_cur, ctx_axes, shift_perm)]
    add x94 -> x0, other arithmetic: 296 us -> none  [the longest x93 296 us: step_body(): return (k_cur, v_cur, dk_cur + dk_part, dv_cur + dv_part, dq_cur + dq_part)]
    dot_general x160 -> x0, matrix products: 276 us -> none  [the longest x32 125 us: block_grads(): jnp.einsum('kqgs,qkgd->ksd', prob_b16, do_blk, preferred_element_type=jnp...]
    pallas_call x0 -> x1, Pallas kernels: none -> 139 us  [local_grads(): pl.pallas_call(functools.partial(grad_kernel, n_row, n_cx, group, scaling...]
    all_to_all x0 -> x3, blocking collectives: none -> 117 us  [the longest x1 65.4 us: local_grads(): rows = lax.all_to_all(send, 'cx', 0, 0, tiled=True)]
    reduce_scatter x0 -> x1, waiting for transfers between devices: none -> 78.4 us  [local_grads(): dkv = lax.psum_scatter(dkv, 'cy', scatter_dimension=0)]
    while x66 -> x0, local copies, waits for them, and re-layouts: 54.6 us -> none
    all_gather x0 -> x1, waiting for transfers between devices: none -> 31.4 us  [local_grads(): kv = lax.all_gather(rows[:, 2 * group:], 'cy', axis=0)]
  transfers between devices with their start and end apart: 126 -> 2, of which waited for: 63 -> 2; matrix products, arithmetic and copies ran while one was open for 29% -> 1% of each run, Pallas kernels for 0% -> 0%
where the time goes in v1:
time: 405 us; the launch traced here: 401 us
  Pallas kernels  139 us (34%)
  blocking collectives  117 us (29%)
  waiting for transfers between devices  110 us (27%)
  local copies, waits for them, and re-layouts  15.7 us (4%)
  between operations  14.2 us (4%)
  other arithmetic  5.36 us (1%)
    pallas_call x1, Pallas kernels, local_grads(): pl.pallas_call(functools.partial(grad_kernel, n_row, n_cx, group, scaling...  139 us
    reduce_scatter x1, waiting for transfers between devices, local_grads(): dkv = lax.psum_scatter(dkv, 'cy', scatter_dimension=0)  78.4 us
    all_to_all x1, blocking collectives, local_grads(): rows = lax.all_to_all(send, 'cx', 0, 0, tiled=True)  65.4 us
    all_to_all x1, blocking collectives, local_grads(): back = lax.all_to_all(back, 'cx', 0, 0, tiled=True)  42.6 us
    all_gather x1, waiting for transfers between devices, local_grads(): kv = lax.all_gather(rows[:, 2 * group:], 'cy', axis=0)  31.4 us
    unnamed x15, local copies, waits for them, and re-layouts  12.9 us
    all_to_all x1, blocking collectives, local_grads(): stats = lax.all_to_all(stats, 'cx', 0, 0, tiled=True)  8.64 us
  transfers between devices with their start and end apart: 2, of which 2 were waited for; matrix products, arithmetic and copies ran while one was open for 1% of the time, Pallas kernels for 0%

profile of v1, /device:TPU:120, one launch (start us, length us, event | category | flops | bytes accessed | tf_op | source)
XLA Modules:
  0.0 400.5 jit_solution(7640296137813953202)
XLA Ops:
  7.3 1.2 copy.27
  8.5 1.1 copy.28
  9.6 2.4 copy.25
  12.0 0.8 copy.26
  12.9 0.9 pad_maximum_fusion
  13.7 65.4 %all_to_all.15.rows_ref = bf16[8,10,2,128,128]{4,3,2,1,0:T(8,128)(2,1)S(1)} all-to-all(bf16[8,10,2,128,128]{4,3,2,1,0:T(8,128)(2,1)S(1)} %pad_maximum_fusion), channel_id=1, replica_groups=mesh['dp'=1,'cy'=4,'cx'=8] {'cx'}, dimensions={0} | all-to-all | bytes 10485760 | tf_op jit(solution)/shard_map/all_to_all | solution.py:123
  79.1 2.4 copy-done
  81.5 1.0 slice.25
  82.6 0.1 reduce-scatter.2.cloned.1.call-start
  82.7 2.8 fusion
  85.5 0.1 copy.38
  85.6 8.6 %all_to_all.16.stats_ref = f32[8,2,8,128]{3,2,1,0:T(8,128)} all-to-all(f32[8,2,8,128]{3,2,1,0:T(8,128)S(1)} %maximum_bitcast_fusion), channel_id=1, replica_groups=mesh['dp'=1,'cy'=4,'cx'=8] {'cx'}, dimensions={0} | all-to-all | bytes 131072 | tf_op jit(solution)/shard_map/all_to_all | solution.py:124
  94.3 31.4 %all-gather.3.cloned.1.call-done = bf16[32,2,2,128,128]{4,3,2,1,0:T(8,128)(2,1)} async-done(((bf16[8,2,2,128,128]{4,3,2,1,0:T(8,128)(2,1)}), bf16[32,2,2,128,128]{4,3,2,1,0:T(8,128)(2,1)}) %all-gather.3.cloned.1.call-update) | async-done | bytes 4194320 | tf_op jit(solution)/shard_map/all_gather | solution.py:125
  125.6 138.6 %grad_kernel.1 = (bf16[8,4,2,128,128]{4,3,2,1,0:T(8,128)(2,1)}, f32[4,8,2,2,128,128]{5,4,3,2,1,0:T(8,128)}) custom-call(bf16[8,10,2,128,128]{4,3,2,1,0:T(8,128)(2,1)} %copy-done, f32[8,2,8,128]{3,2,1,0:T(8,128)} %all_to_all.16.stats_ref, bf16[4,8,2,2,128,128]{5,4,3,2,1,0:T(8,128)(2,1)} %bitcast.32), custom_call_target="tpu_custom_call" | custom-call | tf_op jit(solution)/shard_map/grad_kernel/pallas_call | solution.py:127
  264.3 78.4 %reduce-scatter.2.cloned.1.call-done = f32[1,8,2,2,128,128]{5,4,3,2,1,0:T(8,128)} async-done(((f32[4,8,2,2,128,128]{5,4,3,2,1,0:T(8,128)}), f32[1,8,2,2,128,128]{5,4,3,2,1,0:T(8,128)}) %reduce-scatter.2.cloned.1.call-update) | async-done | bytes 2097168 | tf_op jit(solution)/shard_map/reduce_scatter | solution.py:136
  342.7 1.3 slice.35
  344.0 1.4 fusion.1
  345.4 0.4 pad_maximum_fusion.1
  345.8 42.6 %all_to_all.17 = bf16[8,6,2,128,128]{4,3,2,1,0:T(8,128)(2,1)S(1)} all-to-all(bf16[8,6,2,128,128]{4,3,2,1,0:T(8,128)(2,1)S(1)} %pad_maximum_fusion.1), channel_id=1, replica_groups=mesh['dp'=1,'cy'=4,'cx'=8] {'cx'}, dimensions={0} | all-to-all | bytes 6291456 | tf_op jit(solution)/shard_map/all_to_all | solution.py:140
  388.4 0.2 slice.28
  388.6 2.7 copy.31
  391.3 0.1 fusion.2
  391.4 1.1 copy.33
  392.5 1.1 copy.32
  (16 shorter events, 0.3 us)
Async XLA Ops:
  7.2 4.9 %copy-start.1 = (bf16[256,32,128]{2,1,0:T(8,128)(2,1)S(1)}, bf16[256,32,128]{2,1,0:T(8,128)(2,1)}, u32[]{:S(2)}) copy-start(bf16[256,32,128]{2,1,0:T(8,128)(2,1)} %param.10) | copy-start | bytes 6291460
  7.2 118.4 %all-gather.3.cloned.1.call-start = ((), (), s32[]{:S(2)}) async-start(), calls=%async_computation.5 | async-start | bytes 5242880 | tf_op jit(solution)/shard_map/all_gather | solution.py:125
  79.1 2.4 copy-start
  81.5 1.2 copy-start.3
  82.6 260.1 %reduce-scatter.2.cloned.1.call-start = ((), (), s32[]{:S(2)}) async-start(), calls=%async_computation.4 | async-start | bytes 10485760 | tf_op jit(solution)/shard_map/reduce_scatter | solution.py:136
  264.3 81.1 %copy-start.2 = (bf16[8,4,2,128,128]{4,3,2,1,0:T(8,128)(2,1)S(1)}, bf16[8,4,2,128,128]{4,3,2,1,0:T(8,128)(2,1)}, u32[]{:S(2)}) copy-start(bf16[8,4,2,128,128]{4,3,2,1,0:T(8,128)(2,1)} %get-tuple-element.5) | copy-start | bytes 6291460
Sparse Core Ops, SparseCore 0:
  82.7 42.8 all-gather.2
  264.4 78.2 reduce-scatter.1

commit v2 on v1

v2 whole, which is shorter than its diff:
```python
import functools
import math
import jax
import jax.numpy as jnp
from jax import lax
from jax.experimental import pallas as pl
from jax.experimental.pallas import tpu as pltpu
from jax.sharding import PartitionSpec as P

TK = 256
TQ = 512
KERNEL_VMEM = 48 * 1024 * 1024
LOG2E = 1.4426950408889634


def grad_kernel(n_row, n_src, group, scaling, own, last, src_lo, src_n, rows_ref, stats_ref, kv_ref, *refs):
    if own:
        dqt_ref, dkv_ref = refs
        dqt_ref[...] = jnp.zeros_like(dqt_ref)
    elif last:
        dqt_ref, dq_ref, dkv_ref = refs
    else:
        dqt_in, dqt_ref, dkv_ref = refs
        dqt_ref[...] = dqt_in[...]
    my_row = lax.axis_index('cy')
    tok, dim = rows_ref.shape[3], rows_ref.shape[4]
    k_src = TK // tok
    dkv_ref[...] = jnp.zeros_like(dkv_ref)
    s_mul = jnp.float32(scaling * LOG2E)

    def tile(head, q_half, q_first, q_n, k_at, o_at, k_half, k_n, mask):
        qs = pl.ds(q_first, q_n)
        k_t = kv_ref[k_at + (0, k_half)].reshape(k_n * tok, dim)
        v_t = kv_ref[k_at + (1, k_half)].reshape(k_n * tok, dim)
        q_t = rows_ref[qs, head, q_half].reshape(q_n * tok, dim)
        do_t = rows_ref[qs, group + head, q_half].reshape(q_n * tok, dim)
        lse = jnp.concatenate([stats_ref[q_first + i, q_half, pl.ds(head, 1), :] for i in range(q_n)], axis=1)
        delta = jnp.concatenate([stats_ref[q_first + i, q_half, pl.ds(group + head, 1), :] for i in range(q_n)], axis=1)
        nt = (((1,), (1,)), ((), ()))
        s_t = lax.dot_general(k_t, q_t, nt, preferred_element_type=jnp.float32)
        p_t = jnp.exp2(s_t * s_mul - lse)
        if mask is not None:
            p_t = jnp.where(mask, p_t, 0.0)
        dp_t = lax.dot_general(v_t, do_t, nt, preferred_element_type=jnp.float32)
        ds_t = (p_t * (dp_t - delta)).astype(jnp.bfloat16)
        p_b = p_t.astype(jnp.bfloat16)
        dv = jnp.dot(p_b, do_t, preferred_element_type=jnp.float32)
        dk = jnp.dot(ds_t, q_t, preferred_element_type=jnp.float32)
        dqt = lax.dot_general(k_t, ds_t, (((0,), (0,)), ((), ())), preferred_element_type=jnp.float32)
        dkv_ref[o_at + (0, k_half)] += dk.reshape(k_n, tok, dim)
        dkv_ref[o_at + (1, k_half)] += dv.reshape(k_n, tok, dim)
        lanes = pl.ds(pl.multiple_of(q_first * tok, q_n * tok), q_n * tok)
        dqt_ref[head, q_half, :, lanes] += dqt

    q_n = TQ // tok
    n_qt = n_src // q_n
    n_kt = src_n // k_src
    n_pairs = 1 if own else 2 * (n_row - 1)

    def full_step(idx, carry):
        kt = lax.rem(idx, n_kt)
        head = lax.rem(lax.div(idx, n_kt), group)
        ks = pl.ds(src_lo + kt * k_src, k_src)
        ko = pl.ds(kt * k_src, k_src)
        if own:
            q_half, k_half = 1, 0
            k_at, o_at = (ks,), (ko,)
        else:
            pair = lax.div(idx, n_kt * group)
            other = lax.rem(my_row + 1 + lax.rem(pair, n_row - 1), n_row)
            before = other < my_row
            first = pair < n_row - 1
            q_half = jnp.where(jnp.logical_or(first, jnp.logical_not(before)), 1, 0)
            k_half = jnp.where(jnp.logical_or(first, before), 0, 1)
            k_at, o_at = (other, ks), (other, ko)
        for qt in range(n_qt):
            tile(head, q_half, qt * q_n, q_n, k_at, o_at, k_half, k_src, None)
        return carry

    lax.fori_loop(0, n_pairs * group * n_kt, full_step, 0)

    def diag_step(idx, carry):
        kt = lax.rem(idx, n_kt)
        head = lax.rem(lax.div(idx, n_kt), group)
        half = lax.div(idx, n_kt * group)
        low = jnp.where(half == 0, kt, 0)
        high = jnp.where(half == 0, n_kt, kt + 1)

        def inner(qt, c):
            q_i = lax.broadcasted_iota(jnp.int32, (TK, TK), 1)
            k_i = lax.broadcasted_iota(jnp.int32, (TK, TK), 0)
            q_pc = qt * k_src + q_i // tok
            k_pc = kt * k_src + k_i // tok
            q_pc = jnp.where(half == 0, q_pc, n_src - 1 - q_pc)
            k_pc = jnp.where(half == 0, k_pc, n_src - 1 - k_pc)
            mask = q_pc * tok + lax.rem(q_i, tok) >= k_pc * tok + lax.rem(k_i, tok)
            ks = (pl.ds(kt * k_src, k_src),)
            tile(head, half, qt * k_src, k_src, ks, ks, half, k_src, mask)
            return c

        return lax.fori_loop(low, high, inner, carry)

    if own:
        lax.fori_loop(0, 2 * group * n_kt, diag_step, 0)

    def out_step(idx, carry):
        src = lax.rem(idx, n_src)
        head = lax.rem(lax.div(idx, n_src), group)
        half = lax.div(idx, n_src * group)
        blk = dqt_ref[head, half, :, pl.ds(pl.multiple_of(src * tok, tok), tok)]
        dq_ref[src, head, half] = (jnp.transpose(blk, (1, 0)) * scaling).astype(jnp.bfloat16)
        return carry

    if last:
        lax.fori_loop(0, 2 * group * n_src, out_step, 0)


def solution(mesh):
    n_row = mesh.shape['cy']
    n_cx = mesh.shape['cx']
    row_spec = P(('dp', 'cy', 'cx'), None, None)
    stat_spec = P(('dp', 'cy', 'cx'), None)
    vm = pl.BlockSpec(memory_space=pltpu.VMEM)

    def local_grads(query_rows, key_rows, value_rows, out_rows, grad_out, log_sum_exp):
        tok_dev, n_heads, dim = query_rows.shape
        kv_heads = key_rows.shape[1]
        group = n_heads // kv_heads
        tok = tok_dev // 2
        scaling = 1.0 / math.sqrt(dim)
        assert kv_heads == n_cx
        delta = jnp.einsum('thd,thd->th', grad_out, out_rows, preferred_element_type=jnp.float32)

        def by_head(x, per):
            return x.reshape(2, tok, kv_heads, per, dim).transpose(2, 3, 0, 1, 4)

        kv_own = jnp.concatenate([by_head(key_rows, 1), by_head(value_rows, 1)], axis=1)
        kv_own = lax.all_to_all(kv_own, 'cx', 0, 0, tiled=True)
        kv_all = lax.all_gather(kv_own, 'cy', axis=0)
        send = jnp.concatenate([by_head(query_rows, group), by_head(grad_out, group)], axis=1)
        stats = jnp.concatenate([(log_sum_exp * LOG2E).reshape(2, tok, kv_heads, group), delta.reshape(2, tok, kv_heads, group)], axis=3).transpose(2, 0, 3, 1)
        stats = lax.all_to_all(stats, 'cx', 0, 0, tiled=True)
        rows = lax.all_to_all(send, 'cx', 0, 0, tiled=True)

        dqt_shape = jax.ShapeDtypeStruct((group, 2, dim, n_cx * tok), jnp.float32)

        def call(kv, dqt, own, last, src_lo, src_n):
            src_shape = (src_n, 2, 2, tok, dim)
            dkv_shape = jax.ShapeDtypeStruct(src_shape if own else (n_row,) + src_shape, jnp.float32)
            dq_shape = jax.ShapeDtypeStruct((n_cx, group, 2, tok, dim), jnp.bfloat16) if last else dqt_shape
            pairs = (1 + 2 * 0.625) if own else 2 * (n_row - 1)
            flops = int(10 * pairs * group * dim * (n_cx * tok) * (src_n * tok))
            args = (rows, stats, kv) + (() if own else (dqt,))
            return pl.pallas_call(
                functools.partial(grad_kernel, n_row, n_cx, group, scaling, own, last, src_lo, src_n),
                out_shape=(dq_shape, dkv_shape),
                in_specs=[vm] * len(args),
                out_specs=(vm, vm),
                compiler_params=pltpu.CompilerParams(vmem_limit_bytes=KERNEL_VMEM),
                cost_estimate=pl.CostEstimate(flops=2 * flops, bytes_accessed=16 * 1024 * 1024, transcendentals=0),
                name='grad_own' if own else 'grad_other',
            )(*args)

        def scatter(x):
            return lax.psum_scatter(x, 'cy', scatter_dimension=0)

        half_src = n_cx // 2
        dqt, dkv_own = call(kv_own, None, True, False, 0, n_cx)
        dqt, dkv_a = call(kv_all, dqt, False, False, 0, half_src)
        dkv_a = scatter(dkv_a)
        dq, dkv_b = call(kv_all, dqt, False, True, half_src, half_src)
        dkv_b = scatter(dkv_b)
        dq = lax.all_to_all(dq, 'cx', 0, 0, tiled=True)
        dkv = jnp.concatenate([dkv_a, dkv_b], axis=0) + dkv_own
        dkv = dkv * jnp.array([scaling, 1.0], jnp.float32)[None, :, None, None, None]
        dkv = lax.all_to_all(dkv.astype(jnp.bfloat16), 'cx', 0, 0, tiled=True)

        def by_tok(x):
            return x.transpose(2, 3, 0, 1, 4).reshape(tok_dev, -1, dim)

        return by_tok(dq), by_tok(dkv[:, :1]), by_tok(dkv[:, 1:])

    return jax.shard_map(local_grads, mesh=mesh, in_specs=(row_spec,) * 5 + (stat_spec,), out_specs=(row_spec,) * 3, check_vma=False)
```

time: 405 us -> 374 us (0.923)
  blocking collectives: 117 us -> 54.4 us
  starting transfers between devices: 0.13 us -> 17.2 us
  Pallas kernels: 139 us -> 148 us
  other arithmetic: 5.36 us -> 9.73 us
    all_to_all x2 -> x0, blocking collectives: 51.2 us -> none  [the longest x1 42.6 us: local_grads(): back = lax.all_to_all(back, 'cx', 0, 0, tiled=True)]
    all_gather x1, waiting for transfers between devices: 31.4 us -> 0.01 us  [local_grads(): kv_all = lax.all_gather(kv_own, 'cy', axis=0)]
    all_to_all x0 -> x4, waiting for transfers between devices: none -> 24.8 us  [the longest x1 13.1 us: local_grads(): kv_own = lax.all_to_all(kv_own, 'cx', 0, 0, tiled=True)]
    all_to_all x0 -> x4, starting transfers between devices: none -> 17 us  [the longest x1 4.59 us: local_grads(): kv_own = lax.all_to_all(kv_own, 'cx', 0, 0, tiled=True)]
    all_to_all x1, blocking collectives: 65.4 us -> 54.4 us  [local_grads(): rows = lax.all_to_all(send, 'cx', 0, 0, tiled=True)]
    pallas_call x1 -> x3, Pallas kernels: 139 us -> 148 us  [call(): pl.pallas_call(functools.partial(grad_kernel, n_row, n_cx, group, scaling...]
    reduce_scatter x1 -> x2, waiting for transfers between devices: 78.4 us -> 82.8 us  [scatter(): return lax.psum_scatter(x, 'cy', scatter_dimension=0)]
    unnamed x15 -> x23, local copies, waits for them, and re-layouts: 12.9 us -> 16.6 us
  transfers between devices with their start and end apart: 2 -> 7, of which waited for: 2 -> 4; matrix products, arithmetic and copies ran while one was open for 1% -> 4% of each run, Pallas kernels for 0% -> 14%
where the time goes in v2:
time: 374 us; the launch traced here: 369 us
  Pallas kernels  148 us (40%)
  waiting for transfers between devices  108 us (29%)
  blocking collectives  54.4 us (15%)
  starting transfers between devices  17.2 us (5%)
  local copies, waits for them, and re-layouts  16.8 us (4%)
  between operations  13.9 us (4%)
  other arithmetic  9.73 us (3%)
    pallas_call x3, Pallas kernels, call(): pl.pallas_call(functools.partial(grad_kernel, n_row, n_cx, group, scaling...  148 us
    reduce_scatter x2, waiting for transfers between devices, scatter(): return lax.psum_scatter(x, 'cy', scatter_dimension=0)  82.8 us
    all_to_all x1, blocking collectives, local_grads(): rows = lax.all_to_all(send, 'cx', 0, 0, tiled=True)  54.4 us
    unnamed x23, local copies, waits for them, and re-layouts  16.6 us
    all_to_all x1, waiting for transfers between devices, local_grads(): kv_own = lax.all_to_all(kv_own, 'cx', 0, 0, tiled=True)  13.1 us
    all_to_all x1, waiting for transfers between devices, local_grads(): dkv = lax.all_to_all(dkv.astype(jnp.bfloat16), 'cx', 0, 0, tiled=True)  11.7 us
  transfers between devices with their start and end apart: 7, of which 4 were waited for; matrix products, arithmetic and copies ran while one was open for 4% of the time, Pallas kernels for 14%

profile of v2, /device:TPU:120, one launch (start us, length us, event | category | flops | bytes accessed | tf_op | source)
XLA Modules:
  0.0 368.9 jit_solution(8628692825667235454)
XLA Ops:
  7.2 1.1 copy.30
  8.3 1.1 copy.31
  9.4 1.1 pad_maximum_fusion.1
  10.5 4.6 %all-to-all-start.2 = ((bf16[8,2,2,128,128]{4,3,2,1,0:T(8,128)(2,1)}), bf16[8,2,2,128,128]{4,3,2,1,0:T(8,128)(2,1)S(1)}, u32[]{:S(2)}, u32[]{:S(2)}) async-start(bf16[8,2,2,128,128]{4,3,2,1,0:T(8,128)(2,1)} %pad_maximum_fusion.1), calls=%async_computation.2 | async-start | bytes 2097152 | tf_op jit(solution)/shard_map/all_to_all | solution.py:138
  15.2 2.8 fusion
  17.9 13.1 %all-to-all-done.2.kv_ref = bf16[8,2,2,128,128]{4,3,2,1,0:T(8,128)(2,1)S(1)} async-done(((bf16[8,2,2,128,128]{4,3,2,1,0:T(8,128)(2,1)}), bf16[8,2,2,128,128]{4,3,2,1,0:T(8,128)(2,1)S(1)}, u32[]{:S(2)}, u32[]{:S(2)}) %all-to-all-start.2) | async-done | bytes 1048608 | tf_op jit(solution)/shard_map/all_to_all | solution.py:138
  32.9 3.6 all-to-all-start.1
  36.5 2.7 copy.27
  40.1 2.3 pad_maximum_fusion
  42.4 54.4 %all_to_all.25.rows_ref = bf16[8,8,2,128,128]{4,3,2,1,0:T(8,128)(2,1)} all-to-all(bf16[8,8,2,128,128]{4,3,2,1,0:T(8,128)(2,1)} %pad_maximum_fusion), channel_id=1, replica_groups=mesh['dp'=1,'cy'=4,'cx'=8] {'cx'}, dimensions={0} | all-to-all | bytes 8388608 | tf_op jit(solution)/shard_map/all_to_all | solution.py:143
  96.8 52.1 %grad_own.1 = (f32[4,2,128,1024]{3,2,1,0:T(8,128)}, f32[8,2,2,128,128]{4,3,2,1,0:T(8,128)S(1)}) custom-call(bf16[8,8,2,128,128]{4,3,2,1,0:T(8,128)(2,1)} %all_to_all.25.rows_ref, f32[8,2,8,128]{3,2,1,0:T(8,128)S(1)} %all-to-all-done.1.stats_ref, bf16[8,2,2,128,128]{4,3,2,1,0:T(8,128)(2,1)S(1)} %copy-done.1), custom_call_target="tpu_custom_call" | custom-call | flops 24159191040 | bytes 16777216 | tf_op jit(solution)/shard_map/grad_own/pallas_call | solution.py:154
  148.9 45.1 %grad_other.2 = (f32[4,2,128,1024]{3,2,1,0:T(8,128)S(1)}, f32[4,4,2,2,128,128]{5,4,3,2,1,0:T(8,128)}) custom-call(bf16[8,8,2,128,128]{4,3,2,1,0:T(8,128)(2,1)} %all_to_all.25.rows_ref, f32[8,2,8,128]{3,2,1,0:T(8,128)S(1)} %all-to-all-done.1.stats_ref, bf16[4,8,2,2,128,128]{5,4,3,2,1,0:T(8,128)(2,1)} %bitcast.38, f32[4,2,128,1024]{3,2,1,0:T(8,128)} %get-tuple-element.9.refs_0_), custom_call_target="tpu_custom_call" | custom-call | flops 32212254720 | bytes 16777216 | tf_op jit(solution)/shard_map/grad_other/pallas_call | solution.py:154
  194.0 1.9 copy-done.3
  196.0 51.3 %grad_other.3 = (bf16[8,4,2,128,128]{4,3,2,1,0:T(8,128)(2,1)S(1)}, f32[4,4,2,2,128,128]{5,4,3,2,1,0:T(8,128)}) custom-call(bf16[8,8,2,128,128]{4,3,2,1,0:T(8,128)(2,1)} %all_to_all.25.rows_ref, f32[8,2,8,128]{3,2,1,0:T(8,128)S(1)} %all-to-all-done.1.stats_ref, bf16[4,8,2,2,128,128]{5,4,3,2,1,0:T(8,128)(2,1)} %bitcast.39, f32[4,2,128,1024]{3,2,1,0:T(8,128)} %copy-done.3), custom_call_target="tpu_custom_call" | custom-call | flops 32212254720 | bytes 16777216 | tf_op jit(solution)/shard_map/grad_other/pallas_call | solution.py:154
  247.3 1.3 copy-done.2
  249.5 4.6 %all-to-all-start.3 = ((bf16[8,4,2,128,128]{4,3,2,1,0:T(8,128)(2,1)}), bf16[8,4,2,128,128]{4,3,2,1,0:T(8,128)(2,1)}, u32[]{:S(2)}, u32[]{:S(2)}) async-start(bf16[8,4,2,128,128]{4,3,2,1,0:T(8,128)(2,1)} %copy-done.2), calls=%async_computation.3 | async-start | bytes 4194304 | tf_op jit(solution)/shard_map/all_to_all | solution.py:173
  254.0 36.4 %reduce-scatter.5.cloned.1.call-done = f32[1,4,2,2,128,128]{5,4,3,2,1,0:T(8,128)} async-done(((f32[4,4,2,2,128,128]{5,4,3,2,1,0:T(8,128)}), f32[1,4,2,2,128,128]{5,4,3,2,1,0:T(8,128)}) %reduce-scatter.5.cloned.1.call-update) | async-done | bytes 1048592 | tf_op jit(solution)/shard_map/reduce_scatter | solution.py:165
  290.4 46.4 %reduce-scatter.3.cloned.1.call-done = f32[1,4,2,2,128,128]{5,4,3,2,1,0:T(8,128)} async-done(((f32[4,4,2,2,128,128]{5,4,3,2,1,0:T(8,128)}), f32[1,4,2,2,128,128]{5,4,3,2,1,0:T(8,128)}) %reduce-scatter.3.cloned.1.call-update) | async-done | bytes 1048592 | tf_op jit(solution)/shard_map/reduce_scatter | solution.py:165
  336.8 2.9 fusion.2
  339.8 4.3 %all-to-all-start.4 = ((bf16[8,2,2,128,128]{4,3,2,1,0:T(8,128)(2,1)}), bf16[8,2,2,128,128]{4,3,2,1,0:T(8,128)(2,1)S(1)}, u32[]{:S(2)}, u32[]{:S(2)}) async-start(bf16[8,2,2,128,128]{4,3,2,1,0:T(8,128)(2,1)} %fusion.2), calls=%async_computation.6 | async-start | bytes 2097152 | tf_op jit(solution)/shard_map/all_to_all | solution.py:176
  344.0 4.3 %copy.32 = bf16[256,32,128]{2,1,0:T(8,128)(2,1)} copy(bf16[256,32,128]{2,0,1:T(8,128)(2,1)} %bitcast.11) | data formatting | bytes 4194304
  348.3 11.7 %all-to-all-done.4 = bf16[8,2,2,128,128]{4,3,2,1,0:T(8,128)(2,1)S(1)} async-done(((bf16[8,2,2,128,128]{4,3,2,1,0:T(8,128)(2,1)}), bf16[8,2,2,128,128]{4,3,2,1,0:T(8,128)(2,1)S(1)}, u32[]{:S(2)}, u32[]{:S(2)}) %all-to-all-start.4) | async-done | bytes 1048608 | tf_op jit(solution)/shard_map/all_to_all | solution.py:176
  360.1 1.1 copy.34
  361.2 1.1 copy.33
  (32 shorter events, 3.7 us)
Async XLA Ops:
  9.4 5.7 %copy-start.4 = (bf16[256,32,128]{2,1,0:T(8,128)(2,1)S(1)}, bf16[256,32,128]{2,1,0:T(8,128)(2,1)}, u32[]{:S(2)}) copy-start(bf16[256,32,128]{2,1,0:T(8,128)(2,1)} %param.11) | copy-start | bytes 6291460
  10.5 20.5 %all-to-all-start.2 = ((bf16[8,2,2,128,128]{4,3,2,1,0:T(8,128)(2,1)}), bf16[8,2,2,128,128]{4,3,2,1,0:T(8,128)(2,1)S(1)}, u32[]{:S(2)}, u32[]{:S(2)}) async-start(bf16[8,2,2,128,128]{4,3,2,1,0:T(8,128)(2,1)} %pad_maximum_fusion.1), calls=%async_computation.2 | async-start | bytes 2097152 | tf_op jit(solution)/shard_map/all_to_all | solution.py:138
  15.1 17.0 %copy-start.6 = (f32[256,32]{0,1:T(8,128)S(1)}, f32[256,32]{0,1:T(8,128)}, u32[]{:S(2)}) copy-start(f32[256,32]{0,1:T(8,128)} %param.12) | copy-start | bytes 98308
  15.1 133.8 %all-gather.3.cloned.1.call-start = ((), (), s32[]{:S(2)}) async-start(), calls=%async_computation.9 | async-start | bytes 5242880 | tf_op jit(solution)/shard_map/all_gather | solution.py:139
  31.0 1.0 copy-start
  32.9 9.5 %all-to-all-start.1 = ((f32[8,2,8,128]{3,2,1,0:T(8,128)}), f32[8,2,8,128]{3,2,1,0:T(8,128)S(1)}, u32[]{:S(2)}, u32[]{:S(2)}) async-start(f32[8,2,8,128]{3,2,1,0:T(8,128)} %maximum_bitcast_fusion), calls=%async_computation.1 | async-start | bytes 131072 | tf_op jit(solution)/shard_map/all_to_all | solution.py:142
  36.4 2.8 copy-start.5
  36.4 254.0 %reduce-scatter.5.cloned.1.call-start = ((), (), s32[]{:S(2)}) async-start(), calls=%async_computation.8 | async-start | bytes 5242880 | tf_op jit(solution)/shard_map/reduce_scatter | solution.py:165
  42.4 54.4 %copy-start.1 = (bf16[8,2,2,128,128]{4,3,2,1,0:T(8,128)(2,1)S(1)}, bf16[8,2,2,128,128]{4,3,2,1,0:T(8,128)(2,1)}, u32[]{:S(2)}) copy-start(bf16[8,2,2,128,128]{4,3,2,1,0:T(8,128)(2,1)} %copy-done) | copy-start | bytes 3145732
  194.0 1.9 copy-start.3
  247.3 1.3 copy-start.2
  248.7 88.1 %reduce-scatter.3.cloned.1.call-start = ((), (), s32[]{:S(2)}) async-start(), calls=%async_computation.7 | async-start | bytes 5242880 | tf_op jit(solution)/shard_map/reduce_scatter | solution.py:165
  249.4 87.4 %copy-start.7 = (f32[2]{0:T(128)S(1)}, f32[2]{0:T(128)}, u32[]{:S(2)}) copy-start(f32[2]{0:T(128)} %constant.4.clone) | copy-start | bytes 28
  249.5 90.3 %all-to-all-start.3 = ((bf16[8,4,2,128,128]{4,3,2,1,0:T(8,128)(2,1)}), bf16[8,4,2,128,128]{4,3,2,1,0:T(8,128)(2,1)}, u32[]{:S(2)}, u32[]{:S(2)}) async-start(bf16[8,4,2,128,128]{4,3,2,1,0:T(8,128)(2,1)} %copy-done.2), calls=%async_computation.3 | async-start | bytes 4194304 | tf_op jit(solution)/shard_map/all_to_all | solution.py:173
  339.8 20.2 %all-to-all-start.4 = ((bf16[8,2,2,128,128]{4,3,2,1,0:T(8,128)(2,1)}), bf16[8,2,2,128,128]{4,3,2,1,0:T(8,128)(2,1)S(1)}, u32[]{:S(2)}, u32[]{:S(2)}) async-start(bf16[8,2,2,128,128]{4,3,2,1,0:T(8,128)(2,1)} %fusion.2), calls=%async_computation.6 | async-start | bytes 2097152 | tf_op jit(solution)/shard_map/all_to_all | solution.py:176
Sparse Core Ops, SparseCore 0:
  32.2 42.9 all-gather.2
  248.8 41.5 reduce-scatter.4
  292.7 44.0 reduce-scatter.2
